TPU v7x, 32 devices: a whole 2x2x4 slice. The times are simulated.
32 devices in a mesh: grp: 4 (over z), seq: 4 (over y, core), tp: 2 (over x).
Axes of the slice: x: 2, y: 2, z: 4, core: 2. Of those that a mesh axis runs over, the one named last changes fastest.
Arguments:
- queries: bfloat16 [2048, 8192], P(('grp', 'seq', 'tp')), may hold values from -108 to 108
- key_rows: bfloat16 [2048, 1024], P(('grp', 'seq', 'tp')), may hold values from -4 to 4
- value_rows: bfloat16 [2048, 1024], P(('grp', 'seq', 'tp')), may hold values from -6 to 6
- image_lengths: int32 [4, 4], P('grp'), may hold values from 1 to 256, 512 in all within a row
- block_table: int32 [16, 4], P(('grp', 'seq')), may hold values from 0 to 3, as said below
Outputs:
- attended: bfloat16 [2048, 8192], P(('grp', 'seq'), 'tp')
Inputs may be any that keep to these rules, and one draw needn't show every extreme that they name: `block_table`: for each shard index and each group, exactly one block of each encoder group's shard is destined to that group.
All inputs are finite; a program needn't handle non-finite values.
Results may differ from a plain program's by a relative error of at most 0.004.
Values may be sent and summed in bfloat16 or wider, within the bound.
A program may use at most 64 MiB of HBM per device.

v0:
```python
import functools
import math

import jax
import jax.numpy as jnp
from jax import lax
from jax.experimental import pallas as pl
from jax.experimental.pallas import tpu as pltpu
from jax.sharding import PartitionSpec as P

HD = 128
MASKED = -1e30
MESH = pl.DeviceIdType.MESH


def partner(index, offset, size):
    offset = jnp.int32(offset)
    if size & (size - 1):
        return lax.rem(index + offset, size)
    result = jnp.int32(0)
    weight = 1
    while weight < size:
        mine, other = lax.rem(index // weight, 2), lax.rem(offset // weight, 2)
        result = result + weight * (mine + other - 2 * mine * other)
        weight *= 2
    return result


def kernel(sizes, q_in, k_in, v_in, lengths, table, out, *scratch):
    (groups, shard_count, tps, per, block, q_width, kv_width, pieces, ratio) = sizes
    local_rows = groups * block
    count = len(pieces)
    k_pieces = [j for j in range(count) if pieces[j][0] == 0]
    v_pieces = [j for j in range(count) if pieces[j][0] == 1]
    q_pieces = [j for j in range(count) if pieces[j][0] == 2]
    q_chunks = len(q_pieces)
    starts = [pieces[j][1] for j in q_pieces]
    chunks = [pieces[j][2] for j in q_pieces]
    stage = scratch[0:3]
    gathered = scratch[3 : 3 + count]
    packed = scratch[3 + count : 3 + 2 * count]
    q_recv = scratch[3 + 2 * count : 3 + 2 * count + q_chunks]
    rest = 3 + 2 * count + q_chunks
    (k_all, v_all, obuf, bias_ref) = scratch[rest : rest + 4]
    (load_sem, own_sem, xs_sem, xr_sem, zs_sem, zr_sem, ys_sem, yr_sem, out_sem) = scratch[
        rest + 4 :
    ]
    g = lax.axis_index("grp")
    s = lax.axis_index("seq")
    t = lax.axis_index("tp")

    inputs = (k_in, v_in, q_in)

    def source(j):
        which, offset, width = pieces[j]
        return which, width, offset

    def part_width(which):
        return q_width if which == 2 else kv_width

    loads = [pltpu.make_async_copy(inputs[i], stage[i], load_sem.at[i]) for i in range(3)]
    own = []
    for j in range(count):
        which, width, offset = source(j)
        lanes = pl.ds(pl.multiple_of(t * part_width(which) + offset, HD), width)
        own.append(
            pltpu.make_async_copy(
                inputs[which].at[:, :, lanes],
                gathered[j].at[pl.ds(t * per, per)],
                own_sem.at[j],
            )
        )
    for copy in loads:
        copy.start()
    for copy in own:
        copy.start()

    barrier = pltpu.get_barrier_semaphore()
    for d in range(1, tps):
        pl.semaphore_signal(
            barrier, inc=1, device_id={"tp": partner(t, d, tps)}, device_id_type=MESH
        )
    for d in range(1, shard_count):
        pl.semaphore_signal(
            barrier, inc=1, device_id={"seq": partner(s, d, shard_count)}, device_id_type=MESH
        )
    for d in range(1, groups):
        pl.semaphore_signal(
            barrier, inc=1, device_id={"grp": partner(g, d, groups)}, device_id_type=MESH
        )
    pl.semaphore_wait(barrier, tps + shard_count + groups - 3)

    def x_copy(j, d):
        which, width, offset = source(j)
        peer = partner(t, d, tps)
        lanes = pl.ds(pl.multiple_of(peer * part_width(which) + offset, HD), width)
        return pltpu.make_async_remote_copy(
            src_ref=stage[which].at[:, :, lanes],
            dst_ref=gathered[j].at[pl.ds(t * per, per)],
            send_sem=xs_sem.at[j, d],
            recv_sem=xr_sem.at[j, d],
            device_id={"tp": peer},
            device_id_type=MESH,
        )

    for j in range(count):
        which, offset, _ = pieces[j]
        if offset == 0:
            loads[which].wait()
        for d in range(1, tps):
            x_copy(j, d).start()

    order = list(range(groups - 1, 0, -1))
    chosen = []
    for d in [0] + order:
        dest = partner(g, d, groups)
        pick = jnp.int32(0)
        for b in range(groups):
            pick = jnp.where(table[0, b] == dest, b, pick)
        chosen.append(pick)

    def landing(j, group):
        which, offset, width = pieces[j]
        if which == 2:
            return q_recv[j - q_pieces[0]].at[group]
        return (k_all, v_all)[which].at[s, group, :, pl.ds(offset, width)]

    def z_copy(j, d):
        return pltpu.make_async_remote_copy(
            src_ref=packed[j].at[d],
            dst_ref=landing(j, g),
            send_sem=zs_sem.at[j, d],
            recv_sem=zr_sem.at[j, d],
            device_id={"grp": partner(g, d, groups)},
            device_id_type=MESH,
        )

    def hand_over(j):
        own[j].wait()
        for d in range(1, tps):
            x_copy(j, d).wait_recv()
        for d, pick in zip(order, chosen[1:]):
            packed[j][d] = gathered[j][pick]
        for d in order:
            z_copy(j, d).start()
        landing(j, g)[...] = gathered[j][chosen[0]]

    def arrived(j):
        for d in range(1, groups):
            z_copy(j, d).wait_recv()

    relayed = shard_count % 2 == 0 and shard_count & (shard_count - 1) == 0

    def y_copy(i, d, slot, to):
        whole = (k_all, v_all)[i]
        return pltpu.make_async_remote_copy(
            src_ref=whole.at[slot],
            dst_ref=whole.at[slot],
            send_sem=ys_sem.at[i, d],
            recv_sem=yr_sem.at[i, d],
            device_id={"seq": partner(s, to, shard_count)},
            device_id_type=MESH,
        )

    def direct(d):
        return not relayed or d % 2 == 0 or d == 1

    def y_any(i, d):
        if direct(d):
            return y_copy(i, d, s, d)
        return y_copy(i, d, partner(s, d - 1, shard_count), 1)

    def spread(i):
        for j in (k_pieces, v_pieces)[i]:
            arrived(j)
        for d in range(shard_count - 1, 0, -1):
            if direct(d):
                y_any(i, d).start()

    def relay(i):
        for d in range(shard_count - 1, 0, -1):
            if not direct(d):
                y_any(i, d - 1).wait_recv()
                y_any(i, d).start()

    for j in k_pieces + v_pieces + q_pieces[:1]:
        hand_over(j)

    keys = shard_count * local_rows
    query_pos = s * local_rows + lax.broadcasted_iota(jnp.int32, (local_rows, keys), 0)
    key_pos = lax.broadcasted_iota(jnp.int32, (local_rows, keys), 1)
    query_img = jnp.zeros((local_rows, keys), jnp.int32)
    key_img = jnp.zeros((local_rows, keys), jnp.int32)
    bound = jnp.int32(0)
    for i in range(lengths.shape[1] - 1):
        bound = bound + lengths[0, i]
        query_img = query_img + (query_pos >= bound).astype(jnp.int32)
        key_img = key_img + (key_pos >= bound).astype(jnp.int32)
    visible = (key_pos <= query_pos) & (query_img == key_img)
    bias_ref[...] = jnp.where(visible, 0.0, MASKED)

    spread(0)
    for j in q_pieces[1:3]:
        hand_over(j)
    spread(1)
    for j in q_pieces[3:4]:
        hand_over(j)
    relay(0)
    for j in q_pieces[4:5]:
        hand_over(j)
    relay(1)
    for j in q_pieces[5:]:
        hand_over(j)
    for i in range(2):
        for d in range(1, shard_count):
            if not direct(d) or d == 1 or not relayed:
                y_any(i, d).wait_recv()

    factor = math.log2(math.e) / math.sqrt(HD)

    def out_copy(n):
        return pltpu.make_async_copy(
            obuf.at[:, pl.ds(starts[n], chunks[n])],
            out.at[:, pl.ds(starts[n], chunks[n])],
            out_sem.at[n],
        )

    for n in range(q_chunks):
        arrived(q_pieces[n])
        for r in range(chunks[n] // HD):
            head = starts[n] // HD + r
            kv = head // ratio
            key = k_all[:, :, :, kv * HD : (kv + 1) * HD].reshape(keys, HD)
            value = v_all[:, :, :, kv * HD : (kv + 1) * HD].reshape(keys, HD)
            query = q_recv[n][:, :, r * HD : (r + 1) * HD].reshape(local_rows, HD)
            scores = lax.dot_general(
                query, key, (((1,), (1,)), ((), ())), preferred_element_type=jnp.float32
            )
            masked = scores + bias_ref[...]
            peak = jnp.max(masked, axis=1, keepdims=True)
            weights = jnp.exp2((masked - peak) * factor)
            summed = jnp.sum(weights, axis=1, keepdims=True)
            product = jnp.dot(
                weights.astype(jnp.bfloat16), value, preferred_element_type=jnp.float32
            )
            obuf[:, head * HD : (head + 1) * HD] = (product / summed).astype(jnp.bfloat16)
        out_copy(n).start()

    for j in range(count):
        for d in range(1, tps):
            x_copy(j, d).wait_send()
        for d in range(1, groups):
            z_copy(j, d).wait_send()
    for i in range(2):
        for d in range(1, shard_count):
            y_any(i, d).wait_send()
    for n in range(q_chunks):
        out_copy(n).wait()


def chunk_widths(heads, step):
    return [HD * min(step, heads - at) for at in range(0, heads, step)]


def growing(width):
    pieces = []
    at, size = 0, HD
    while at < width:
        size = min(size, width - at)
        pieces.append((at, size))
        at += size
        size = at
    return pieces


def shards(queries, key_rows, value_rows, image_lengths, block_table):
    groups, shard_count, tps = (lax.axis_size(a) for a in ("grp", "seq", "tp"))
    rows, q_total = queries.shape
    kv_total = key_rows.shape[1]
    local_rows = rows * tps
    block = local_rows // groups
    per = rows // block
    q_width, kv_width = q_total // tps, kv_total // tps
    ratio = q_total // kv_total
    chunks = chunk_widths(q_width // HD, max(1, ratio // 2))
    q_chunks = len(chunks)
    pieces = [(0, a, w) for a, w in growing(kv_width)]
    pieces.append((1, 0, kv_width))
    pieces += [(2, sum(chunks[:n]), w) for n, w in enumerate(chunks)]
    count = len(pieces)
    sizes = (groups, shard_count, tps, per, block, q_width, kv_width, tuple(pieces), ratio)
    bf16 = jnp.bfloat16
    widths = [w for _, _, w in pieces]
    dma = pltpu.SemaphoreType.DMA
    scratch = (
        [pltpu.VMEM((per, block, w), bf16) for w in (kv_total, kv_total, q_total)]
        + [pltpu.VMEM((groups, block, w), bf16) for w in widths]
        + [pltpu.VMEM((groups, block, w), bf16) for w in widths]
        + [pltpu.VMEM((groups, block, w), bf16) for w in chunks]
        + [
            pltpu.VMEM((shard_count, groups, block, kv_width), bf16),
            pltpu.VMEM((shard_count, groups, block, kv_width), bf16),
            pltpu.VMEM((local_rows, q_width), bf16),
            pltpu.VMEM((local_rows, shard_count * local_rows), jnp.float32),
            dma((3,)),
            dma((count,)),
            dma((count, tps)),
            dma((count, tps)),
            dma((count, groups)),
            dma((count, groups)),
            dma((2, shard_count)),
            dma((2, shard_count)),
            dma((q_chunks,)),
        ]
    )
    hbm = pl.BlockSpec(memory_space=pl.ANY)
    smem = pl.BlockSpec(memory_space=pltpu.SMEM)
    return pl.pallas_call(
        functools.partial(kernel, sizes),
        out_shape=jax.ShapeDtypeStruct((local_rows, q_width), bf16),
        in_specs=[hbm, hbm, hbm, smem, smem],
        out_specs=hbm,
        scratch_shapes=scratch,
        compiler_params=pltpu.CompilerParams(collective_id=0, has_side_effects=True),
    )(
        queries.reshape(per, block, q_total),
        key_rows.reshape(per, block, kv_total),
        value_rows.reshape(per, block, kv_total),
        image_lengths,
        block_table,
    )


def solution(mesh):
    in_specs = (
        P(("grp", "seq", "tp"), None),
        P(("grp", "seq", "tp"), None),
        P(("grp", "seq", "tp"), None),
        P("grp", None),
        P(("grp", "seq"), None),
    )
    out_specs = P(("grp", "seq"), "tp")
    return jax.shard_map(shards, mesh=mesh, in_specs=in_specs, out_specs=out_specs, check_vma=False)
```

profile of v0, /device:TPU:0, one launch (start us, length us, event | category | flops | bytes accessed | tf_op | source)
XLA Modules:
  0.0 44.6 jit_solution(141719236783567638)
XLA Ops:
  0.0 42.3 %shard_map.55 = bf16[128,4096]{1,0:T(8,128)(2,1)} custom-call(bf16[2,32,8192]{2,1,0:T(8,128)(2,1)} %bitcast.3, bf16[2,32,1024]{2,1,0:T(8,128)(2,1)} %bitcast.4, bf16[2,32,1024]{2,1,0:T(8,128)(2,1)} %bitcast.5, s32[1,4]{1,0:T(1,128)} %lengths.1, s32[1,4]{1,0:T(1,128)} %table.1), custom_call_target="tpu_custom_call" | custom-call | tf_op jit(solution)/shard_map/pallas_call | solution.py:318
  42.3 2.3 %copy.7 = bf16[128,4096]{1,0:T(8,128)(2,1)} copy(bf16[128,4096]{1,0:T(8,128)(2,1)} %shard_map.55) | data formatting | bytes 2097152
where the time goes:
time: 44.7 us; the launch traced here: 44.6 us
  Pallas kernels  42.3 us (95%)
  local copies, waits for them, and re-layouts  2.29 us (5%)
    pallas_call x1, Pallas kernels, shards(): pl.pallas_call(functools.partial(kernel, sizes), out_shape=jax.ShapeDtype...  42.3 us
    unnamed x1, local copies, waits for them, and re-layouts  2.29 us

commit v1 on v0

--- a/solution.py
+++ b/solution.py
@@ -110,7 +110,8 @@
         for d in range(1, tps):
             x_copy(j, d).start()
 
-    order = list(range(groups - 1, 0, -1))
+    order = list(range(1, groups))
+    held_back = [d for d in order if d >= 3 * groups // 4]
     chosen = []
     for d in [0] + order:
         dest = partner(g, d, groups)
@@ -142,7 +143,8 @@
         for d, pick in zip(order, chosen[1:]):
             packed[j][d] = gathered[j][pick]
         for d in order:
-            z_copy(j, d).start()
+            if j not in q_pieces or d not in held_back:
+                z_copy(j, d).start()
         landing(j, g)[...] = gathered[j][chosen[0]]
 
     def arrived(j):
@@ -211,6 +213,9 @@
     relay(1)
     for j in q_pieces[5:]:
         hand_over(j)
+    for j in q_pieces:
+        for d in held_back:
+            z_copy(j, d).start()
     for i in range(2):
         for d in range(1, shard_count):
             if not direct(d) or d == 1 or not relayed:

time: 44.7 us -> 46.2 us (1.034)
  the two profiles are of different devices: /device:TPU:0 before, /device:TPU:8 now
where the time goes in v1:
time: 46.2 us; the launch traced here: 46.1 us
  Pallas kernels  43.8 us (95%)
  local copies, waits for them, and re-layouts  2.29 us (5%)
    pallas_call x1, Pallas kernels, shards(): pl.pallas_call(functools.partial(kernel, sizes), out_shape=jax.ShapeDtype...  43.8 us
    unnamed x1, local copies, waits for them, and re-layouts  2.29 us

profile of v1, /device:TPU:8, one launch (start us, length us, event | category | flops | bytes accessed | tf_op | source)
XLA Modules:
  0.0 46.1 jit_solution(5402139226792212506)
XLA Ops:
  0.0 43.8 %shard_map.55 = bf16[128,4096]{1,0:T(8,128)(2,1)} custom-call(bf16[2,32,8192]{2,1,0:T(8,128)(2,1)} %bitcast.3, bf16[2,32,1024]{2,1,0:T(8,128)(2,1)} %bitcast.4, bf16[2,32,1024]{2,1,0:T(8,128)(2,1)} %bitcast.5, s32[1,4]{1,0:T(1,128)} %lengths.1, s32[1,4]{1,0:T(1,128)} %table.1), custom_call_target="tpu_custom_call" | custom-call | tf_op jit(solution)/shard_map/pallas_call | solution.py:323
  43.8 2.3 %copy.7 = bf16[128,4096]{1,0:T(8,128)(2,1)} copy(bf16[128,4096]{1,0:T(8,128)(2,1)} %shard_map.55) | data formatting | bytes 2097152

commit v2 on v1

--- a/solution.py
+++ b/solution.py
@@ -243,12 +243,12 @@
             )
             masked = scores + bias_ref[...]
             peak = jnp.max(masked, axis=1, keepdims=True)
-            weights = jnp.exp2((masked - peak) * factor)
-            summed = jnp.sum(weights, axis=1, keepdims=True)
-            product = jnp.dot(
-                weights.astype(jnp.bfloat16), value, preferred_element_type=jnp.float32
+            weights = jnp.exp2((masked - peak) * factor).astype(jnp.bfloat16)
+            extended = jnp.concatenate([value, jnp.ones_like(value)], axis=1)
+            product = jnp.dot(weights, extended, preferred_element_type=jnp.float32)
+            obuf[:, head * HD : (head + 1) * HD] = (product[:, :HD] / product[:, HD:]).astype(
+                jnp.bfloat16
             )
-            obuf[:, head * HD : (head + 1) * HD] = (product / summed).astype(jnp.bfloat16)
         out_copy(n).start()
 
     for j in range(count):

time: 46.2 us -> 42.2 us (0.913)
  Pallas kernels: 43.8 us -> 39.8 us
    pallas_call x1, Pallas kernels: 43.8 us -> 39.8 us  [shards(): pl.pallas_call(functools.partial(kernel, sizes), out_shape=jax.ShapeDtype...]
where the time goes in v2:
time: 42.2 us; the launch traced here: 42.1 us
  Pallas kernels  39.8 us (94%)
  local copies, waits for them, and re-layouts  2.29 us (5%)
    pallas_call x1, Pallas kernels, shards(): pl.pallas_call(functools.partial(kernel, sizes), out_shape=jax.ShapeDtype...  39.8 us
    unnamed x1, local copies, waits for them, and re-layouts  2.29 us

profile of v2, /device:TPU:8, one launch (start us, length us, event | category | flops | bytes accessed | tf_op | source)
XLA Modules:
  0.0 42.1 jit_solution(16797209793919313201)
XLA Ops:
  0.0 39.8 %shard_map.55 = bf16[128,4096]{1,0:T(8,128)(2,1)} custom-call(bf16[2,32,8192]{2,1,0:T(8,128)(2,1)} %bitcast.3, bf16[2,32,1024]{2,1,0:T(8,128)(2,1)} %bitcast.4, bf16[2,32,1024]{2,1,0:T(8,128)(2,1)} %bitcast.5, s32[1,4]{1,0:T(1,128)} %lengths.1, s32[1,4]{1,0:T(1,128)} %table.1), custom_call_target="tpu_custom_call" | custom-call | tf_op jit(solution)/shard_map/pallas_call | solution.py:323
  39.8 2.3 %copy.7 = bf16[128,4096]{1,0:T(8,128)(2,1)} copy(bf16[128,4096]{1,0:T(8,128)(2,1)} %shard_map.55) | data formatting | bytes 2097152

commit v3 on v2

--- a/solution.py
+++ b/solution.py
@@ -41,10 +41,8 @@
     packed = scratch[3 + count : 3 + 2 * count]
     q_recv = scratch[3 + 2 * count : 3 + 2 * count + q_chunks]
     rest = 3 + 2 * count + q_chunks
-    (k_all, v_all, obuf, bias_ref) = scratch[rest : rest + 4]
-    (load_sem, own_sem, xs_sem, xr_sem, zs_sem, zr_sem, ys_sem, yr_sem, out_sem) = scratch[
-        rest + 4 :
-    ]
+    (k_all, v_all, bias_ref) = scratch[rest : rest + 3]
+    (load_sem, own_sem, xs_sem, xr_sem, zs_sem, zr_sem, ys_sem, yr_sem) = scratch[rest + 3 :]
     g = lax.axis_index("grp")
     s = lax.axis_index("seq")
     t = lax.axis_index("tp")
@@ -222,13 +220,6 @@
                 y_any(i, d).wait_recv()
 
     factor = math.log2(math.e) / math.sqrt(HD)
-
-    def out_copy(n):
-        return pltpu.make_async_copy(
-            obuf.at[:, pl.ds(starts[n], chunks[n])],
-            out.at[:, pl.ds(starts[n], chunks[n])],
-            out_sem.at[n],
-        )
 
     for n in range(q_chunks):
         arrived(q_pieces[n])
@@ -246,10 +237,9 @@
             weights = jnp.exp2((masked - peak) * factor).astype(jnp.bfloat16)
             extended = jnp.concatenate([value, jnp.ones_like(value)], axis=1)
             product = jnp.dot(weights, extended, preferred_element_type=jnp.float32)
-            obuf[:, head * HD : (head + 1) * HD] = (product[:, :HD] / product[:, HD:]).astype(
+            out[:, head * HD : (head + 1) * HD] = (product[:, :HD] / product[:, HD:]).astype(
                 jnp.bfloat16
             )
-        out_copy(n).start()
 
     for j in range(count):
         for d in range(1, tps):
@@ -259,8 +249,6 @@
     for i in range(2):
         for d in range(1, shard_count):
             y_any(i, d).wait_send()
-    for n in range(q_chunks):
-        out_copy(n).wait()
 
 
 def chunk_widths(heads, step):
@@ -305,7 +293,6 @@
         + [
             pltpu.VMEM((shard_count, groups, block, kv_width), bf16),
             pltpu.VMEM((shard_count, groups, block, kv_width), bf16),
-            pltpu.VMEM((local_rows, q_width), bf16),
             pltpu.VMEM((local_rows, shard_count * local_rows), jnp.float32),
             dma((3,)),
             dma((count,)),
@@ -315,16 +302,15 @@
             dma((count, groups)),
             dma((2, shard_count)),
             dma((2, shard_count)),
-            dma((q_chunks,)),
         ]
     )
     hbm = pl.BlockSpec(memory_space=pl.ANY)
     smem = pl.BlockSpec(memory_space=pltpu.SMEM)
     return pl.pallas_call(
         functools.partial(kernel, sizes),
-        out_shape=jax.ShapeDtypeStruct((local_rows, q_width), bf16),
+        out_shape=pltpu.VMEM((local_rows, q_width), bf16),
         in_specs=[hbm, hbm, hbm, smem, smem],
-        out_specs=hbm,
+        out_specs=pl.BlockSpec(memory_space=pltpu.VMEM),
         scratch_shapes=scratch,
         compiler_params=pltpu.CompilerParams(collective_id=0, has_side_effects=True),
     )(

time: 42.2 us -> 40.3 us (0.955)
  local copies, waits for them, and re-layouts: 2.29 us -> 0.97 us
  Pallas kernels: 39.8 us -> 39.1 us
    unnamed x1, local copies, waits for them, and re-layouts: 2.29 us -> 0.97 us
    pallas_call x1, Pallas kernels: 39.8 us -> 39.1 us  [shards(): pl.pallas_call(functools.partial(kernel, sizes), out_shape=pltpu.VMEM((lo...]
where the time goes in v3:
time: 40.3 us; the launch traced here: 40.1 us
  Pallas kernels  39.1 us (97%)
  local copies, waits for them, and re-layouts  0.97 us (2%)
    pallas_call x1, Pallas kernels, shards(): pl.pallas_call(functools.partial(kernel, sizes), out_shape=pltpu.VMEM((lo...  39.1 us
    unnamed x1, local copies, waits for them, and re-layouts  0.97 us

profile of v3, /device:TPU:8, one launch (start us, length us, event | category | flops | bytes accessed | tf_op | source)
XLA Modules:
  0.0 40.1 jit_solution(14237937468358110756)
XLA Ops:
  0.0 39.1 %shard_map.55 = bf16[128,4096]{1,0:T(8,128)(2,1)S(1)} custom-call(bf16[2,32,8192]{2,1,0:T(8,128)(2,1)} %bitcast.3, bf16[2,32,1024]{2,1,0:T(8,128)(2,1)} %bitcast.4, bf16[2,32,1024]{2,1,0:T(8,128)(2,1)} %bitcast.5, s32[1,4]{1,0:T(1,128)} %lengths.1, s32[1,4]{1,0:T(1,128)} %table.1), custom_call_target="tpu_custom_call" | custom-call | tf_op jit(solution)/shard_map/pallas_call | solution.py:309
  39.1 1.0 %copy.7 = bf16[128,4096]{1,0:T(8,128)(2,1)} copy(bf16[128,4096]{1,0:T(8,128)(2,1)S(1)} %shard_map.55) | data formatting | bytes 2097152

commit v4 on v3

--- a/solution.py
+++ b/solution.py
@@ -24,6 +24,10 @@
         result = result + weight * (mine + other - 2 * mine * other)
         weight *= 2
     return result
+
+
+def origin(index, offset, size):
+    return partner(index, size - offset if size & (size - 1) else offset, size)
 
 
 def kernel(sizes, q_in, k_in, v_in, lengths, table, out, *scratch):
@@ -42,7 +46,9 @@
     q_recv = scratch[3 + 2 * count : 3 + 2 * count + q_chunks]
     rest = 3 + 2 * count + q_chunks
     (k_all, v_all, bias_ref) = scratch[rest : rest + 3]
-    (load_sem, own_sem, xs_sem, xr_sem, zs_sem, zr_sem, ys_sem, yr_sem) = scratch[rest + 3 :]
+    (load_sem, own_sem, xs_sem, xr_sem, zs_sem, zr_sem, ys_sem, yr_sem, in_sem) = scratch[
+        rest + 3 :
+    ]
     g = lax.axis_index("grp")
     s = lax.axis_index("seq")
     t = lax.axis_index("tp")
@@ -73,20 +79,56 @@
     for copy in own:
         copy.start()
 
+    relayed = shard_count % 2 == 0 and shard_count & (shard_count - 1) == 0
+
+    def direct(d):
+        return not relayed or d % 2 == 0 or d == 1
+
+    seq_peers = [d for d in range(1, shard_count) if direct(d)]
+    sides = [side for side in (1, -1) if groups > 1]
+
+    def beyond(side):
+        return groups - 1 - g if side == 1 else g
+
     barrier = pltpu.get_barrier_semaphore()
     for d in range(1, tps):
         pl.semaphore_signal(
             barrier, inc=1, device_id={"tp": partner(t, d, tps)}, device_id_type=MESH
         )
-    for d in range(1, shard_count):
+    for d in seq_peers:
         pl.semaphore_signal(
             barrier, inc=1, device_id={"seq": partner(s, d, shard_count)}, device_id_type=MESH
         )
-    for d in range(1, groups):
-        pl.semaphore_signal(
-            barrier, inc=1, device_id={"grp": partner(g, d, groups)}, device_id_type=MESH
-        )
-    pl.semaphore_wait(barrier, tps + shard_count + groups - 3)
+    for side in sides:
+
+        @pl.when(beyond(side) >= 1)
+        def _(side=side):
+            pl.semaphore_signal(
+                barrier, inc=1, device_id={"grp": g + side}, device_id_type=MESH
+            )
+
+    met = jnp.int32(tps - 1 + len(seq_peers))
+    for side in sides:
+        met = met + (beyond(side) >= 1).astype(jnp.int32)
+    pl.semaphore_wait(barrier, met)
+
+    def pass_on(side, hops):
+        @pl.when((beyond(side) >= hops) & (beyond(-side) >= 1))
+        def _():
+            pl.semaphore_signal(
+                in_sem.at[(1 - side) // 2, hops + 1],
+                inc=1,
+                device_id={"grp": g - side},
+                device_id_type=MESH,
+            )
+
+    def hear(side, hops):
+        @pl.when(beyond(side) >= hops)
+        def _():
+            pl.semaphore_wait(in_sem.at[(1 - side) // 2, hops], 1)
+
+    for side in sides:
+        pass_on(side, 1)
 
     def x_copy(j, d):
         which, width, offset = source(j)
@@ -108,6 +150,12 @@
         for d in range(1, tps):
             x_copy(j, d).start()
 
+    for hops in range(2, groups):
+        for side in sides:
+            hear(side, hops)
+        for side in sides:
+            pass_on(side, hops)
+
     order = list(range(1, groups))
     held_back = [d for d in order if d >= 3 * groups // 4]
     chosen = []
@@ -118,16 +166,16 @@
             pick = jnp.where(table[0, b] == dest, b, pick)
         chosen.append(pick)
 
-    def landing(j, group):
+    def landing(j, d):
         which, offset, width = pieces[j]
         if which == 2:
-            return q_recv[j - q_pieces[0]].at[group]
-        return (k_all, v_all)[which].at[s, group, :, pl.ds(offset, width)]
+            return q_recv[j - q_pieces[0]].at[d]
+        return (k_all, v_all)[which].at[s, g, :, pl.ds(offset, width)]
 
     def z_copy(j, d):
         return pltpu.make_async_remote_copy(
             src_ref=packed[j].at[d],
-            dst_ref=landing(j, g),
+            dst_ref=landing(j, d),
             send_sem=zs_sem.at[j, d],
             recv_sem=zr_sem.at[j, d],
             device_id={"grp": partner(g, d, groups)},
@@ -143,13 +191,11 @@
         for d in order:
             if j not in q_pieces or d not in held_back:
                 z_copy(j, d).start()
-        landing(j, g)[...] = gathered[j][chosen[0]]
-
-    def arrived(j):
-        for d in range(1, groups):
+        landing(j, 0)[...] = gathered[j][chosen[0]]
+
+    def arrived(j, offsets=range(1, groups)):
+        for d in offsets:
             z_copy(j, d).wait_recv()
-
-    relayed = shard_count % 2 == 0 and shard_count & (shard_count - 1) == 0
 
     def y_copy(i, d, slot, to):
         whole = (k_all, v_all)[i]
@@ -162,9 +208,6 @@
             device_id_type=MESH,
         )
 
-    def direct(d):
-        return not relayed or d % 2 == 0 or d == 1
-
     def y_any(i, d):
         if direct(d):
             return y_copy(i, d, s, d)
@@ -183,11 +226,11 @@
                 y_any(i, d - 1).wait_recv()
                 y_any(i, d).start()
 
-    for j in k_pieces + v_pieces + q_pieces[:1]:
-        hand_over(j)
-
     keys = shard_count * local_rows
-    query_pos = s * local_rows + lax.broadcasted_iota(jnp.int32, (local_rows, keys), 0)
+    row = lax.broadcasted_iota(jnp.int32, (block, keys), 0)
+    query_pos = jnp.concatenate(
+        [s * local_rows + origin(g, d, groups) * block + row for d in range(groups)], axis=0
+    )
     key_pos = lax.broadcasted_iota(jnp.int32, (local_rows, keys), 1)
     query_img = jnp.zeros((local_rows, keys), jnp.int32)
     key_img = jnp.zeros((local_rows, keys), jnp.int32)
@@ -199,21 +242,15 @@
     visible = (key_pos <= query_pos) & (query_img == key_img)
     bias_ref[...] = jnp.where(visible, 0.0, MASKED)
 
-    spread(0)
-    for j in q_pieces[1:3]:
-        hand_over(j)
-    spread(1)
-    for j in q_pieces[3:4]:
-        hand_over(j)
-    relay(0)
-    for j in q_pieces[4:5]:
-        hand_over(j)
-    relay(1)
-    for j in q_pieces[5:]:
+    for j in k_pieces + v_pieces + q_pieces:
         hand_over(j)
     for j in q_pieces:
         for d in held_back:
             z_copy(j, d).start()
+    spread(0)
+    spread(1)
+    relay(0)
+    relay(1)
     for i in range(2):
         for d in range(1, shard_count):
             if not direct(d) or d == 1 or not relayed:
@@ -221,25 +258,56 @@
 
     factor = math.log2(math.e) / math.sqrt(HD)
 
+    def attend(query, head, bias):
+        lanes = slice(head // ratio * HD, (head // ratio + 1) * HD)
+        key = k_all[:, :, :, lanes].reshape(keys, HD)
+        value = v_all[:, :, :, lanes].reshape(keys, HD)
+        scores = lax.dot_general(
+            query, key, (((1,), (1,)), ((), ())), preferred_element_type=jnp.float32
+        )
+        masked = scores + bias
+        peak = jnp.max(masked, axis=1, keepdims=True)
+        weights = jnp.exp2((masked - peak) * factor).astype(jnp.bfloat16)
+        extended = jnp.concatenate([value, jnp.ones_like(value)], axis=1)
+        product = jnp.dot(weights, extended, preferred_element_type=jnp.float32)
+        return (product[:, :HD] / product[:, HD:]).astype(jnp.bfloat16)
+
+    def place(d, head, result):
+        rows = pl.ds(pl.multiple_of(origin(g, d, groups) * block, block), block)
+        out[rows, head * HD : (head + 1) * HD] = result
+
+    prompt = [d for d in range(groups) if d not in held_back]
     for n in range(q_chunks):
-        arrived(q_pieces[n])
+        arrived(q_pieces[n], prompt[1:])
         for r in range(chunks[n] // HD):
             head = starts[n] // HD + r
-            kv = head // ratio
-            key = k_all[:, :, :, kv * HD : (kv + 1) * HD].reshape(keys, HD)
-            value = v_all[:, :, :, kv * HD : (kv + 1) * HD].reshape(keys, HD)
-            query = q_recv[n][:, :, r * HD : (r + 1) * HD].reshape(local_rows, HD)
-            scores = lax.dot_general(
-                query, key, (((1,), (1,)), ((), ())), preferred_element_type=jnp.float32
+            query = q_recv[n][: len(prompt), :, r * HD : (r + 1) * HD]
+            result = attend(
+                query.reshape(len(prompt) * block, HD), head, bias_ref[: len(prompt) * block]
             )
-            masked = scores + bias_ref[...]
-            peak = jnp.max(masked, axis=1, keepdims=True)
-            weights = jnp.exp2((masked - peak) * factor).astype(jnp.bfloat16)
-            extended = jnp.concatenate([value, jnp.ones_like(value)], axis=1)
-            product = jnp.dot(weights, extended, preferred_element_type=jnp.float32)
-            out[:, head * HD : (head + 1) * HD] = (product[:, :HD] / product[:, HD:]).astype(
-                jnp.bfloat16
-            )
+            for d in prompt:
+                place(d, head, result[d * block : (d + 1) * block])
+
+    batches = [range(n, min(n + 2, q_chunks)) for n in range(0, q_chunks, 2)]
+    for batch in batches:
+        for n in batch:
+            arrived(q_pieces[n], held_back)
+        spans = {}
+        for n in batch:
+            for r in range(chunks[n] // HD):
+                head = starts[n] // HD + r
+                spans.setdefault(head // ratio, []).append((n, r, head))
+        for d in held_back:
+            for members in spans.values():
+                stack = [q_recv[n][d, :, r * HD : (r + 1) * HD] for n, r, _ in members]
+                bias = bias_ref[d * block : (d + 1) * block]
+                result = attend(
+                    jnp.concatenate(stack, axis=0),
+                    members[0][2],
+                    jnp.concatenate([bias] * len(members), axis=0),
+                )
+                for i, (_, _, head) in enumerate(members):
+                    place(d, head, result[i * block : (i + 1) * block])
 
     for j in range(count):
         for d in range(1, tps):
@@ -302,6 +370,7 @@
             dma((count, groups)),
             dma((2, shard_count)),
             dma((2, shard_count)),
+            pltpu.SemaphoreType.REGULAR((2, groups + 1)),
         ]
     )
     hbm = pl.BlockSpec(memory_space=pl.ANY)

time: 40.3 us -> 39.1 us (0.970)
  Pallas kernels: 39.1 us -> 37.7 us
    pallas_call x1, Pallas kernels: 39.1 us -> 37.7 us  [shards(): pl.pallas_call(functools.partial(kernel, sizes), out_shape=pltpu.VMEM((lo...]
where the time goes in v4:
time: 39.1 us; the launch traced here: 38.7 us
  Pallas kernels  37.7 us (96%)
  local copies, waits for them, and re-layouts  0.97 us (2%)
    pallas_call x1, Pallas kernels, shards(): pl.pallas_call(functools.partial(kernel, sizes), out_shape=pltpu.VMEM((lo...  37.7 us
    unnamed x1, local copies, waits for them, and re-layouts  0.97 us

profile of v4, /device:TPU:8, one launch (start us, length us, event | category | flops | bytes accessed | tf_op | source)
XLA Modules:
  0.0 38.7 jit_solution(12397774991956016679)
XLA Ops:
  0.0 37.7 %shard_map.55 = bf16[128,4096]{1,0:T(8,128)(2,1)S(1)} custom-call(bf16[2,32,8192]{2,1,0:T(8,128)(2,1)} %bitcast.3, bf16[2,32,1024]{2,1,0:T(8,128)(2,1)} %bitcast.4, bf16[2,32,1024]{2,1,0:T(8,128)(2,1)} %bitcast.5, s32[1,4]{1,0:T(1,128)} %lengths.1, s32[1,4]{1,0:T(1,128)} %table.1), custom_call_target="tpu_custom_call" | custom-call | tf_op jit(solution)/shard_map/pallas_call | solution.py:378
  37.7 1.0 %copy.7 = bf16[128,4096]{1,0:T(8,128)(2,1)} copy(bf16[128,4096]{1,0:T(8,128)(2,1)S(1)} %shard_map.55) | data formatting | bytes 2097152

commit v5 on v4

--- a/solution.py
+++ b/solution.py
@@ -156,8 +156,8 @@
         for side in sides:
             pass_on(side, hops)
 
-    order = list(range(1, groups))
-    held_back = [d for d in order if d >= 3 * groups // 4]
+    held_back = [d for d in range(1, groups) if d >= 3 * groups // 4]
+    order = [d for d in range(groups - 1, 0, -1) if d not in held_back] + held_back
     chosen = []
     for d in [0] + order:
         dest = partner(g, d, groups)

time: 39.1 us -> 38.9 us (level)
  no operation moved by 1% of the time
where the time goes in v5:
time: 38.9 us; the launch traced here: 38.6 us
  Pallas kernels  37.6 us (97%)
  local copies, waits for them, and re-layouts  0.97 us (2%)
    pallas_call x1, Pallas kernels, shards(): pl.pallas_call(functools.partial(kernel, sizes), out_shape=pltpu.VMEM((lo...  37.6 us
    unnamed x1, local copies, waits for them, and re-layouts  0.97 us

profile of v5, /device:TPU:8, one launch (start us, length us, event | category | flops | bytes accessed | tf_op | source)
XLA Modules:
  0.0 38.6 jit_solution(4159020618645081187)
XLA Ops:
  0.0 37.6 %shard_map.55 = bf16[128,4096]{1,0:T(8,128)(2,1)S(1)} custom-call(bf16[2,32,8192]{2,1,0:T(8,128)(2,1)} %bitcast.3, bf16[2,32,1024]{2,1,0:T(8,128)(2,1)} %bitcast.4, bf16[2,32,1024]{2,1,0:T(8,128)(2,1)} %bitcast.5, s32[1,4]{1,0:T(1,128)} %lengths.1, s32[1,4]{1,0:T(1,128)} %table.1), custom_call_target="tpu_custom_call" | custom-call | tf_op jit(solution)/shard_map/pallas_call | solution.py:378
  37.6 1.0 %copy.7 = bf16[128,4096]{1,0:T(8,128)(2,1)} copy(bf16[128,4096]{1,0:T(8,128)(2,1)S(1)} %shard_map.55) | data formatting | bytes 2097152

commit v6 on v5

--- a/solution.py
+++ b/solution.py
@@ -330,7 +330,7 @@
         size = min(size, width - at)
         pieces.append((at, size))
         at += size
-        size = at
+        size = width - at
     return pieces
 
 

time: 38.9 us -> 39 us (level)
  no operation moved by 1% of the time
where the time goes in v6:
time: 39 us; the launch traced here: 38.6 us
  Pallas kernels  37.6 us (96%)
  local copies, waits for them, and re-layouts  0.97 us (2%)
    pallas_call x1, Pallas kernels, shards(): pl.pallas_call(functools.partial(kernel, sizes), out_shape=pltpu.VMEM((lo...  37.6 us
    unnamed x1, local copies, waits for them, and re-layouts  0.97 us

profile of v6, /device:TPU:8, one launch (start us, length us, event | category | flops | bytes accessed | tf_op | source)
XLA Modules:
  0.0 38.6 jit_solution(3729951998082067448)
XLA Ops:
  0.0 37.6 %shard_map.55 = bf16[128,4096]{1,0:T(8,128)(2,1)S(1)} custom-call(bf16[2,32,8192]{2,1,0:T(8,128)(2,1)} %bitcast.3, bf16[2,32,1024]{2,1,0:T(8,128)(2,1)} %bitcast.4, bf16[2,32,1024]{2,1,0:T(8,128)(2,1)} %bitcast.5, s32[1,4]{1,0:T(1,128)} %lengths.1, s32[1,4]{1,0:T(1,128)} %table.1), custom_call_target="tpu_custom_call" | custom-call | tf_op jit(solution)/shard_map/pallas_call | solution.py:378
  37.6 1.0 %copy.7 = bf16[128,4096]{1,0:T(8,128)(2,1)} copy(bf16[128,4096]{1,0:T(8,128)(2,1)S(1)} %shard_map.55) | data formatting | bytes 2097152
